TPU v7x, 8 devices: a whole 2x2x1 slice. The times are simulated.
8 devices in a mesh: dp: 2 (over z, y), ep: 4 (over x, core).
Axes of the slice: x: 2, y: 2, z: 1, core: 2. Of those that a mesh axis runs over, the one named last changes fastest.
Arguments:
- tokens: bfloat16 [2048, 1024], P(('dp', 'ep'))
- w_router: bfloat16 [1024, 32], replicated
- w_gate: bfloat16 [32, 1024, 512], P('ep')
- w_up: bfloat16 [32, 1024, 512], P('ep')
- w_down: bfloat16 [32, 512, 1024], P('ep')
- top_ids: int32 [2048, 8], P(('dp', 'ep'))
- r_proj: bfloat16 [2048, 1024], P(('dp', 'ep'))
Outputs:
- output 1: float32 [2048, 1024], P(('dp', 'ep'))
- output 2: float32 [2048, 1024], P(('dp', 'ep'))
- output 3: float32 [32, 1024, 512], P('ep')
- output 4: float32 [32, 1024, 512], P('ep')
- output 5: float32 [32, 512, 1024], P('ep')
- output 6: float32 [1024, 32], replicated
All inputs are finite; a program needn't handle non-finite values.
Results may differ from a plain program's by a relative error of at most 0.00173.
Values are sent between devices in bfloat16 or wider.
A program may use at most 1 GiB of HBM per device.

v0:
```python
import jax
import jax.numpy as jnp
from jax import lax
from jax.sharding import PartitionSpec as P


def rows_times_wt(lhs_rows, weight, group_sizes):
    dim_nums = lax.RaggedDotDimensionNumbers(dot_dimension_numbers=(([1], [2]), ([], [])), lhs_ragged_dimensions=[0], rhs_group_dimensions=[0])
    return lax.ragged_dot_general(lhs_rows, weight, group_sizes, dim_nums, preferred_element_type=jnp.float32)


def grouped_outer(lhs_rows, rhs_rows, group_sizes):
    dim_nums = lax.RaggedDotDimensionNumbers(dot_dimension_numbers=(([0], [0]), ([], [])), lhs_ragged_dimensions=[0], rhs_group_dimensions=[])
    return lax.ragged_dot_general(lhs_rows, rhs_rows, group_sizes, dim_nums, preferred_element_type=jnp.float32)


def expert_forward(tok_sorted, w_gate, w_up, w_down, group_sizes):
    h_gate = lax.ragged_dot(tok_sorted, w_gate, group_sizes, preferred_element_type=jnp.float32)
    h_up = lax.ragged_dot(tok_sorted, w_up, group_sizes, preferred_element_type=jnp.float32)
    act_rows = (jax.nn.silu(h_gate) * h_up).astype(jnp.bfloat16)
    out_rows = lax.ragged_dot(act_rows, w_down, group_sizes, preferred_element_type=jnp.float32).astype(jnp.bfloat16)
    return out_rows, h_gate, h_up, act_rows


def expert_backward(tok_sorted, d_out, h_gate, h_up, act_rows, w_gate, w_up, w_down, group_sizes):
    d_act = rows_times_wt(d_out, w_down, group_sizes)
    sig_gate = jax.nn.sigmoid(h_gate)
    d_hgate = (d_act * h_up * sig_gate * (1.0 + h_gate * (1.0 - sig_gate))).astype(jnp.bfloat16)
    d_hup = (d_act * h_gate * sig_gate).astype(jnp.bfloat16)
    grad_gate = grouped_outer(tok_sorted, d_hgate, group_sizes)
    grad_up = grouped_outer(tok_sorted, d_hup, group_sizes)
    grad_down = grouped_outer(act_rows, d_out, group_sizes)
    d_rows = (rows_times_wt(d_hgate, w_gate, group_sizes) + rows_times_wt(d_hup, w_up, group_sizes)).astype(jnp.bfloat16)
    return d_rows, grad_gate, grad_up, grad_down


def router_gates(tokens, w_router, top_ids):
    logits = jnp.dot(tokens, w_router, preferred_element_type=jnp.float32)
    return jax.nn.softmax(jnp.take_along_axis(logits, top_ids, axis=1), axis=-1)


def router_backward(tokens, w_router, top_ids, gate_prob, out_asg, d_y):
    n_exp = w_router.shape[1]
    d_gates = jnp.einsum('tkh,th->tk', out_asg, d_y, preferred_element_type=jnp.float32)
    d_sel = gate_prob * (d_gates - jnp.sum(gate_prob * d_gates, axis=-1, keepdims=True))
    onehot = (top_ids[:, :, None] == jnp.arange(n_exp, dtype=jnp.int32)[None, None, :]).astype(jnp.float32)
    d_logit = jnp.einsum('tk,tke->te', d_sel, onehot).astype(jnp.bfloat16)
    grad_router = lax.dot_general(tokens, d_logit, (((0,), (0,)), ((), ())), preferred_element_type=jnp.float32)
    dx_router = lax.dot_general(d_logit, w_router, (((1,), (1,)), ((), ())), preferred_element_type=jnp.float32)
    return grad_router, dx_router


def solution(mesh):
    ep_size = mesh.shape['ep']
    all_axes = ('dp', 'ep')

    def local_step(tokens, w_router, w_gate, w_up, w_down, top_ids, r_proj):
        n_local, hidden = tokens.shape
        top_n = top_ids.shape[1]
        n_exp = w_router.shape[1]
        local_exp = w_gate.shape[0]
        cap_rows = n_local * top_n
        n_slots = ep_size * cap_rows
        gate_prob = router_gates(tokens, w_router, top_ids)
        exp_flat = top_ids.reshape(-1)
        sort_idx = jnp.argsort(exp_flat, stable=True).astype(jnp.int32)
        sorted_exp = exp_flat[sort_idx]
        exp_count = jnp.bincount(exp_flat, length=n_exp).astype(jnp.int32)
        dest_cnt = exp_count.reshape(ep_size, local_exp).sum(axis=1)
        dest_start = jnp.cumsum(dest_cnt) - dest_cnt
        dest_of = sorted_exp // local_exp
        slot_sorted = dest_of * cap_rows + jnp.arange(cap_rows, dtype=jnp.int32) - dest_start[dest_of]
        slot_of_asg = jnp.zeros((cap_rows,), jnp.int32).at[sort_idx].set(slot_sorted)
        slot_ids = jnp.arange(n_slots, dtype=jnp.int32)
        slot_peer = slot_ids // cap_rows
        slot_pos = slot_ids % cap_rows
        send_valid = (slot_pos < dest_cnt[slot_peer])[:, None]
        send_asg = sort_idx[jnp.minimum(dest_start[slot_peer] + slot_pos, cap_rows - 1)]
        send_rows = jnp.where(send_valid, tokens[send_asg // top_n], 0)

        recv_cnt = lax.all_to_all(exp_count.reshape(ep_size, local_exp), 'ep', 0, 0, tiled=True)
        recv_rows = lax.all_to_all(send_rows, 'ep', 0, 0, tiled=True)

        recv_tot = recv_cnt.sum(axis=1)
        group_sizes = recv_cnt.sum(axis=0).astype(jnp.int32)
        grp_end = jnp.cumsum(group_sizes)
        grp_start = grp_end - group_sizes
        src_end = jnp.cumsum(recv_cnt, axis=0)
        src_start = src_end - recv_cnt
        within_start = jnp.cumsum(recv_cnt, axis=1) - recv_cnt
        row_valid = slot_ids < grp_end[-1]
        row_exp = jnp.minimum(jnp.sum((grp_end[None, :] <= slot_ids[:, None]).astype(jnp.int32), axis=1), local_exp - 1)
        row_off = slot_ids - grp_start[row_exp]
        row_src = jnp.minimum(jnp.sum((src_end.T[row_exp] <= row_off[:, None]).astype(jnp.int32), axis=1), ep_size - 1)
        slot_raw = row_src * cap_rows + within_start[row_src, row_exp] + row_off - src_start[row_src, row_exp]
        row_slot = jnp.where(row_valid, slot_raw, 0)
        slot_row = jnp.zeros((n_slots,), jnp.int32).at[jnp.where(row_valid, slot_raw, n_slots)].set(slot_ids, mode='drop')
        slot_valid = (slot_pos < recv_tot[slot_peer])[:, None]
        tok_sorted = jnp.where(row_valid[:, None], recv_rows[row_slot], 0)

        out_sorted, h_gate, h_up, act_rows = expert_forward(tok_sorted, w_gate, w_up, w_down, group_sizes)
        back_rows = lax.all_to_all(jnp.where(slot_valid, out_sorted[slot_row], 0), 'ep', 0, 0, tiled=True)
        out_asg = back_rows[slot_of_asg].reshape(n_local, top_n, hidden)
        d_y = r_proj.astype(jnp.float32)
        y_out = tokens.astype(jnp.float32) + jnp.einsum('tkh,tk->th', out_asg, gate_prob, preferred_element_type=jnp.float32)

        grad_router, dx_router = router_backward(tokens, w_router, top_ids, gate_prob, out_asg, d_y)
        d_out = (gate_prob[:, :, None] * d_y[:, None, :]).astype(jnp.bfloat16).reshape(cap_rows, hidden)
        recv_dout = lax.all_to_all(jnp.where(send_valid, d_out[send_asg], 0), 'ep', 0, 0, tiled=True)
        d_sorted = jnp.where(row_valid[:, None], recv_dout[row_slot], 0)
        d_rows, grad_gate, grad_up, grad_down = expert_backward(tok_sorted, d_sorted, h_gate, h_up, act_rows, w_gate, w_up, w_down, group_sizes)
        d_back = lax.all_to_all(jnp.where(slot_valid, d_rows[slot_row], 0), 'ep', 0, 0, tiled=True)
        d_expert = jnp.sum(d_back[slot_of_asg].reshape(n_local, top_n, hidden), axis=1, dtype=jnp.float32)
        grad_tokens = d_y + dx_router + d_expert
        grad_gate = lax.psum(grad_gate, 'dp')
        grad_up = lax.psum(grad_up, 'dp')
        grad_down = lax.psum(grad_down, 'dp')
        grad_router = lax.psum(grad_router, all_axes)
        return y_out, grad_tokens, grad_gate, grad_up, grad_down, grad_router

    tok_spec = P(all_axes, None)
    exp_spec = P('ep', None, None)
    return jax.shard_map(local_step, mesh=mesh, in_specs=(tok_spec, P(), exp_spec, exp_spec, exp_spec, tok_spec, tok_spec), out_specs=(tok_spec, tok_spec, exp_spec, exp_spec, exp_spec, P()), check_vma=False)
```

profile of v0, /device:TPU:0, one launch (start us, length us, event | category | flops | bytes accessed | tf_op | source)
XLA Modules:
  0.0 2320.7 jit_solution(8452440341691515095)
XLA Ops:
  8.2 14.7 scatter_custom_fusion
  23.5 4.6 all-to-all-start
  30.6 2.6 compare_select_fusion.5
  33.3 5.0 sort.17
  38.4 45.5 %gather_fusion = s32[8192]{0:T(1024)S(1)} fusion(s32[2048]{0:T(1024)S(1)} %get-tuple-element.7, s32[8192]{0:T(1024)S(1)} %broadcast_clamp_fusion.4), kind=kCustom, calls=%fused_computation | custom fusion | bytes 98304 | tf_op jit(solution)/shard_map/gather | solution.py:78
  84.7 35.2 %gather_fusion.1 = bf16[8192,1024]{1,0:T(8,128)(2,1)} fusion(bf16[256,1024]{1,0:T(8,128)(2,1)S(1)} %copy-done.3, s32[8192]{0:T(1024)S(1)} %broadcast_clamp_fusion.2), kind=kCustom, calls=%fused_computation.1 | custom fusion | bytes 33587200 | tf_op jit(solution)/shard_map/gather | solution.py:79
  121.2 5.1 select_reduce_fusion
  127.0 14.1 broadcast_select_fusion.3
  141.1 7.1 all-to-all-start.1
  152.0 5.0 iota_subtract_fusion
  157.0 28.0 %gather_fusion.2 = s32[8192,4]{1,0:T(8,128)} fusion(s32[8,4]{1,0:T(8,128)S(1)} %bitcast.99, s32[8192]{0:T(1024)S(1)} %get-tuple-element.59), kind=kCustom, calls=%fused_computation.2 | custom fusion | bytes 294912 | tf_op jit(solution)/shard_map/gather | solution.py:94
  185.0 4.4 convert_reduce_fusion.1
  189.6 34.3 %gather_fusion.4 = s32[8192]{0:T(1024)S(1)} fusion(s32[4,8]{0,1:T(8,128)S(1)} %sub.98, s32[8192]{0:T(1024)S(1)} %bitcast.100), kind=kCustom, calls=%fused_computation.4 | custom fusion | bytes 131072 | tf_op jit(solution)/shard_map/gather | solution.py:95
  223.9 68.6 %gather_fusion.3 = s32[8192]{0:T(1024)S(1)} fusion(s32[4,8]{1,0:T(4,128)S(1)} %sub.96, s32[8192]{0:T(1024)S(1)} %bitcast.101), kind=kCustom, calls=%fused_computation.3 | custom fusion | bytes 131072 | tf_op jit(solution)/shard_map/gather | solution.py:95
  293.3 30.5 %scatter_custom_fusion.1 = s32[8192]{0:T(1024)S(1)} fusion(s32[8192]{0:T(1024)S(1)} %bitcast.133, s32[8192]{0:T(1024)S(1)} %iota.78, s32[]{:T(128)} %constant.97.clone.1), kind=kCustom, calls=%fused_computation.104 | custom fusion | bytes 32772 | tf_op jit(solution)/shard_map/scatter | solution.py:97
  325.9 5.0 all-to-all-done.1
  330.9 48.4 %gather_fusion.5 = bf16[8192,1024]{1,0:T(8,128)(2,1)} fusion(bf16[8192,1024]{1,0:T(8,128)(2,1)} %bitcast.21, s32[8192]{0:T(1024)S(1)} %broadcast_clamp_fusion), kind=kCustom, calls=%fused_computation.5 | custom fusion | bytes 33587200 | tf_op jit(solution)/shard_map/gather | solution.py:99
  379.3 14.1 broadcast_select_fusion.1
  393.4 15.4 ragged-dot-none.7
  408.8 15.8 ragged-dot-none.8
  424.6 15.0 multiply_convert_fusion.2
  439.6 15.8 ragged-dot-none.6
  455.4 17.5 convert_element_type.52
  472.9 48.4 %gather_fusion.6 = bf16[8192,1024]{1,0:T(8,128)(2,1)} fusion(bf16[8192,1024]{1,0:T(8,128)(2,1)} %convert_element_type.52, s32[8192]{0:T(1024)S(1)} %fusion.11), kind=kCustom, calls=%fused_computation.6 | custom fusion | bytes 33587200 | tf_op jit(solution)/shard_map/gather | solution.py:102
  521.4 14.0 broadcast_select_fusion.5
  535.4 15.8 all-to-all-start.2
  551.8 16.8 gather_fusion.13
  568.8 11.8 gather_fusion.7
  580.7 2.6 compare_select_fusion.15
  583.3 8.2 scatter_custom_fusion.2
  591.6 142.3 %all-to-all-done.2 = bf16[4,2048,1024]{2,1,0:T(8,128)(2,1)} async-done(((bf16[4,2048,1024]{2,1,0:T(8,128)(2,1)}), bf16[4,2048,1024]{2,1,0:T(8,128)(2,1)}, u32[]{:S(2)}, u32[]{:S(2)}) %all-to-all-start.2) | async-done | bytes 16777248 | tf_op jit(solution)/shard_map/all_to_all | solution.py:102
  734.0 18.9 gather_fusion.8
  752.8 4.8 fusion.1
  758.0 2.3 fusion
  760.4 43.2 %gather_fusion.9 = bf16[8192,1024]{1,0:T(8,128)(2,1)} fusion(bf16[2048,1024]{1,0:T(8,128)(2,1)} %fusion, s32[8192]{0:T(1024)S(1)} %broadcast_clamp_fusion.3), kind=kCustom, calls=%fused_computation.9 | custom fusion | bytes 33587200 | tf_op jit(solution)/shard_map/gather | solution.py:109
  803.6 14.0 broadcast_select_fusion.2
  817.6 7.0 all-to-all-start.3
  824.7 11.4 copy.69
  836.1 1.7 ragged-dot-metadata
  840.1 168.7 %all-to-all-done.3 = bf16[4,2048,1024]{2,1,0:T(8,128)(2,1)} async-done(((bf16[4,2048,1024]{2,1,0:T(8,128)(2,1)}), bf16[4,2048,1024]{2,1,0:T(8,128)(2,1)}, u32[]{:S(2)}, u32[]{:S(2)}) %all-to-all-start.3) | async-done | bytes 16777248 | tf_op jit(solution)/shard_map/all_to_all | solution.py:109
  1008.8 48.4 %gather_fusion.10 = bf16[8192,1024]{1,0:T(8,128)(2,1)} fusion(bf16[8192,1024]{1,0:T(8,128)(2,1)} %bitcast.58, s32[8192]{0:T(1024)S(1)} %copy-done.18), kind=kCustom, calls=%fused_computation.10 | custom fusion | bytes 33587200 | tf_op jit(solution)/shard_map/gather | solution.py:110
  1057.2 14.0 broadcast_select_fusion
  1071.2 15.5 ragged-dot-none.5
  1086.8 23.3 %multiply_convert_fusion = (bf16[8192,512]{1,0:T(8,128)(2,1)}, bf16[8192,512]{1,0:T(8,128)(2,1)}) fusion(f32[8192,512]{1,0:T(8,128)} %ragged-dot-none.5, f32[8192,512]{1,0:T(8,128)} %ragged-dot-none.8, f32[8192,512]{1,0:T(8,128)} %ragged-dot-none.7), kind=kLoop, calls=%fused_computation.18 | loop fusion | flops 54525952 | bytes 67108864 | tf_op jit(solution)/shard_map/convert_element_type | solution.py:29
  1110.1 19.5 ragged-dot-none
  1129.6 19.5 ragged-dot-none.1
  1149.1 19.5 ragged-dot-none.2
  1168.7 11.4 copy.70
  1180.1 11.4 copy.71
  1191.4 15.8 ragged-dot-none.4
  1207.3 15.9 ragged-dot-none.3
  1223.1 27.6 %add_convert_fusion = bf16[8192,1024]{1,0:T(8,128)(2,1)} fusion(f32[8192,1024]{1,0:T(8,128)} %ragged-dot-none.4, f32[8192,1024]{1,0:T(8,128)} %ragged-dot-none.3), kind=kLoop, calls=%fused_computation.17 | loop fusion | flops 16777216 | bytes 83886080 | tf_op jit(solution)/shard_map/convert_element_type | solution.py:33
  1250.8 48.4 %gather_fusion.11 = bf16[8192,1024]{1,0:T(8,128)(2,1)} fusion(bf16[8192,1024]{1,0:T(8,128)(2,1)} %add_convert_fusion, s32[8192]{0:T(1024)S(1)} %copy-done.16), kind=kCustom, calls=%fused_computation.11 | custom fusion | bytes 33587200 | tf_op jit(solution)/shard_map/gather | solution.py:112
  1299.2 14.1 broadcast_select_fusion.4
  1313.3 29.8 %all-to-all-start.4 = ((bf16[4,2048,1024]{2,1,0:T(8,128)(2,1)}), bf16[4,2048,1024]{2,1,0:T(8,128)(2,1)}, u32[]{:S(2)}, u32[]{:S(2)}) async-start(bf16[4,2048,1024]{2,1,0:T(8,128)(2,1)} %broadcast_select_fusion.4), calls=%async_computation.4 | async-start | bytes 33554432 | tf_op jit(solution)/shard_map/all_to_all | solution.py:112
  1343.3 3.4 fusion.3
  1348.0 177.8 %all-to-all-done.4 = bf16[4,2048,1024]{2,1,0:T(8,128)(2,1)} async-done(((bf16[4,2048,1024]{2,1,0:T(8,128)(2,1)}), bf16[4,2048,1024]{2,1,0:T(8,128)(2,1)}, u32[]{:S(2)}, u32[]{:S(2)}) %all-to-all-start.4) | async-done | bytes 16777248 | tf_op jit(solution)/shard_map/all_to_all | solution.py:112
  1525.8 18.9 gather_fusion.12
  1544.8 5.5 convert_reduce_fusion
  1551.5 727.6 %all-reduce.6.cloned.1.call-done = (f32[8,1024,512]{2,1,0:T(8,128)}, f32[8,1024,512]{2,1,0:T(8,128)}, f32[8,512,1024]{2,1,0:T(8,128)}) async-done(((f32[8,1024,512]{2,1,0:T(8,128)}, f32[8,1024,512]{2,1,0:T(8,128)}, f32[8,512,1024]{2,1,0:T(8,128)}), (f32[8,1024,512]{2,1,0:T(8,128)}, f32[8,1024,512]{2,1,0:T(8,128)}, f32[8,512,1024]{2,1,0:T(8,128)})) %all-reduce.6.cloned.1.call-update) | async-done | bytes 50331664 | tf_op jit(solution)/shard_map/psum | solution.py:115
  2279.1 13.5 copy.85
  2292.6 2.9 copy-done.8
  2295.6 8.5 copy.86
  2306.6 6.2 copy.87
  (149 shorter events, 23.2 us)
Async XLA Ops:
  7.2 544.3 %copy-start = (bf16[1024,32]{0,1:T(8,128)(2,1)S(1)}, bf16[1024,32]{0,1:T(8,128)(2,1)}, u32[]{:S(2)}) copy-start(bf16[1024,32]{0,1:T(8,128)(2,1)} %param.8) | copy-start | bytes 196612
  23.5 96.5 %all-to-all-start = ((s32[4,1,8]{2,1,0:T(1,128)}), s32[4,1,8]{2,1,0:T(1,128)S(1)}, u32[]{:S(2)}, u32[]{:S(2)}) async-start(s32[4,1,8]{2,1,0:T(1,128)} %bitcast), calls=%async_computation | async-start | bytes 4096 | tf_op jit(solution)/shard_map/all_to_all | solution.py:81
  29.0 9.3 copy-start.11
  33.3 5.1 copy-start.6
  38.4 45.6 %copy-start.1 = (s32[2048]{0:T(1024)}, s32[2048]{0:T(1024)S(1)}, u32[]{:S(2)}) copy-start(s32[2048]{0:T(1024)S(1)} %get-tuple-element.7) | copy-start | bytes 24580
  38.4 46.4 %copy-start.3 = (bf16[256,1024]{1,0:T(8,128)(2,1)S(1)}, bf16[256,1024]{1,0:T(8,128)(2,1)}, u32[]{:S(2)}) copy-start(bf16[256,1024]{1,0:T(8,128)(2,1)} %param.7) | copy-start | bytes 1572868
  126.4 0.6 copy-start.26
  141.1 9.1 copy-start.32
  141.1 189.8 %all-to-all-start.1 = ((bf16[4,2048,1024]{2,1,0:T(8,128)(2,1)}), bf16[4,2048,1024]{2,1,0:T(8,128)(2,1)}, u32[]{:S(2)}, u32[]{:S(2)}) async-start(bf16[4,2048,1024]{2,1,0:T(8,128)(2,1)} %broadcast_select_fusion.3), calls=%async_computation.1 | async-start | bytes 33554432 | tf_op jit(solution)/shard_map/all_to_all | solution.py:82
  324.5 54.8 %copy-start.30 = (pred[8192]{0:T(1024)(128)(4,1)}, pred[8192]{0:T(1024)(128)(4,1)S(1)}, u32[]{:S(2)}) copy-start(pred[8192]{0:T(1024)(128)(4,1)S(1)} %iota_compare_fusion.3) | copy-start | bytes 24580
  324.5 148.4 %copy-start.15 = (s32[8192]{0:T(1024)}, s32[8192]{0:T(1024)S(1)}, u32[]{:S(2)}) copy-start(s32[8192]{0:T(1024)S(1)} %fusion.11) | copy-start | bytes 98308
  325.3 54.1 %copy-start.17 = (s32[8192]{0:T(1024)}, s32[8192]{0:T(1024)S(1)}, u32[]{:S(2)}) copy-start(s32[8192]{0:T(1024)S(1)} %broadcast_clamp_fusion) | copy-start | bytes 98308
  472.9 48.4 %copy-start.24 = (pred[4,2048]{1,0:T(4,128)(4,1)S(1)}, pred[4,2048]{1,0:T(4,128)(4,1)}, u32[]{:S(2)}) copy-start(pred[4,2048]{1,0:T(4,128)(4,1)} %fusion.23) | copy-start | bytes 24580
  535.4 15.8 copy-start.19
  535.4 16.1 copy-start.4
  535.4 198.6 %all-to-all-start.2 = ((bf16[4,2048,1024]{2,1,0:T(8,128)(2,1)}), bf16[4,2048,1024]{2,1,0:T(8,128)(2,1)}, u32[]{:S(2)}, u32[]{:S(2)}) async-start(bf16[4,2048,1024]{2,1,0:T(8,128)(2,1)} %broadcast_select_fusion.5), calls=%async_computation.2 | async-start | bytes 33554432 | tf_op jit(solution)/shard_map/all_to_all | solution.py:102
  551.7 17.0 copy-start.2
  551.8 17.0 copy-start.7
  551.8 28.8 %copy-start.9 = (bf16[256,1024]{1,0:T(8,128)(2,1)S(1)}, bf16[256,1024]{1,0:T(8,128)(2,1)}, u32[]{:S(2)}) copy-start(bf16[256,1024]{1,0:T(8,128)(2,1)} %param.13) | copy-start | bytes 1572868
  551.8 39.8 %copy-start.20 = (s32[8192,1]{0,1:T(1,128)S(1)}, s32[8192,1]{0,1:T(1,128)}, u32[]{:S(2)}) copy-start(s32[8192,1]{0,1:T(1,128)} %get-tuple-element.57) | copy-start | bytes 98308
  591.6 161.3 %copy-start.28 = (s32[2048]{0:T(1024)}, s32[2048]{0:T(1024)S(1)}, u32[]{:S(2)}) copy-start(s32[2048]{0:T(1024)S(1)} %fusion.28) | copy-start | bytes 24580
  757.8 80.0 %copy-start.21 = (f32[256,8]{0,1:T(8,128)}, f32[256,8]{0,1:T(8,128)S(1)}, u32[]{:S(2)}) copy-start(f32[256,8]{0,1:T(8,128)S(1)} %get-tuple-element.50) | copy-start | bytes 24580
  760.4 43.2 %copy-start.27 = (pred[4,2048]{1,0:T(4,128)(4,1)S(1)}, pred[4,2048]{1,0:T(4,128)(4,1)}, u32[]{:S(2)}) copy-start(pred[4,2048]{1,0:T(4,128)(4,1)} %copy-done.26) | copy-start | bytes 24580
  817.6 191.2 %all-to-all-start.3 = ((bf16[4,2048,1024]{2,1,0:T(8,128)(2,1)}), bf16[4,2048,1024]{2,1,0:T(8,128)(2,1)}, u32[]{:S(2)}, u32[]{:S(2)}) async-start(bf16[4,2048,1024]{2,1,0:T(8,128)(2,1)} %broadcast_select_fusion.2), calls=%async_computation.3 | async-start | bytes 33554432 | tf_op jit(solution)/shard_map/all_to_all | solution.py:109
  824.6 13.4 copy-start.12
  824.6 184.2 %copy-start.18 = (s32[8192]{0:T(1024)S(1)}, s32[8192]{0:T(1024)}, u32[]{:S(2)}) copy-start(s32[8192]{0:T(1024)} %copy-done.17) | copy-start | bytes 98308
  824.6 726.9 %all-reduce.4.cloned.1.call-start = ((), (), s32[]{:S(2)}) async-start(), calls=%async_computation.5 | async-start | bytes 262144 | tf_op jit(solution)/shard_map/psum | solution.py:118
  838.5 0.7 copy-start.13
  840.1 1439.1 %all-reduce.6.cloned.1.call-start = ((), (), s32[]{:S(2)}) async-start(), calls=%async_computation.6 | async-start | bytes 100663296 | tf_op jit(solution)/shard_map/psum | solution.py:115
  1008.8 48.4 %copy-start.31 = (pred[8192]{0:T(1024)(128)(4,1)S(1)}, pred[8192]{0:T(1024)(128)(4,1)}, u32[]{:S(2)}) copy-start(pred[8192]{0:T(1024)(128)(4,1)} %copy-done.30) | copy-start | bytes 24580
  1223.1 27.6 %copy-start.16 = (s32[8192]{0:T(1024)S(1)}, s32[8192]{0:T(1024)}, u32[]{:S(2)}) copy-start(s32[8192]{0:T(1024)} %copy-done.15) | copy-start | bytes 98308
  1250.7 48.4 %copy-start.25 = (pred[4,2048]{1,0:T(4,128)(4,1)S(1)}, pred[4,2048]{1,0:T(4,128)(4,1)}, u32[]{:S(2)}) copy-start(pred[4,2048]{1,0:T(4,128)(4,1)} %fusion.23) | copy-start | bytes 24580
  1313.3 29.9 %copy-start.22 = (f32[256,8]{0,1:T(8,128)S(1)}, f32[256,8]{0,1:T(8,128)}, u32[]{:S(2)}) copy-start(f32[256,8]{0,1:T(8,128)} %copy-done.21) | copy-start | bytes 24580
  1313.3 33.4 %copy-start.5 = (bf16[256,1024]{1,0:T(8,128)(2,1)S(1)}, bf16[256,1024]{1,0:T(8,128)(2,1)}, u32[]{:S(2)}) copy-start(bf16[256,1024]{1,0:T(8,128)(2,1)} %param.7) | copy-start | bytes 1572868
  1313.3 212.6 %copy-start.29 = (s32[2048]{0:T(1024)S(1)}, s32[2048]{0:T(1024)}, u32[]{:S(2)}) copy-start(s32[2048]{0:T(1024)} %copy-done.28) | copy-start | bytes 24580
  1313.3 212.6 %all-to-all-start.4 = ((bf16[4,2048,1024]{2,1,0:T(8,128)(2,1)}), bf16[4,2048,1024]{2,1,0:T(8,128)(2,1)}, u32[]{:S(2)}, u32[]{:S(2)}) async-start(bf16[4,2048,1024]{2,1,0:T(8,128)(2,1)} %broadcast_select_fusion.4), calls=%async_computation.4 | async-start | bytes 33554432 | tf_op jit(solution)/shard_map/all_to_all | solution.py:112
  1525.8 24.4 %copy-start.10 = (bf16[256,1024]{1,0:T(8,128)(2,1)S(1)}, bf16[256,1024]{1,0:T(8,128)(2,1)}, u32[]{:S(2)}) copy-start(bf16[256,1024]{1,0:T(8,128)(2,1)} %param.13) | copy-start | bytes 1572868
  1525.8 24.4 %copy-start.14 = (f32[256,1,32]{2,1,0:T(1,128)S(1)}, f32[256,1,32]{2,1,0:T(1,128)}, u32[]{:S(2)}) copy-start(f32[256,1,32]{2,1,0:T(1,128)} %copy-done.13) | copy-start | bytes 98308
  2279.1 16.4 copy-start.8
  2279.1 24.9 %slice-start = ((s8[16777216]{0:T(1024)(128)(4,1)}), s8[4194304]{0:T(1024)(128)(4,1)S(1)}, s32[]{:S(2)}) async-start(s8[16777216]{0:T(1024)(128)(4,1)} %bitcast.109), calls=%async_computation.7 | async-start | bytes 8388608
  2279.1 24.9 %slice-start.1 = ((s8[16777216]{0:T(1024)(128)(4,1)}), s8[4194304]{0:T(1024)(128)(4,1)S(1)}, s32[]{:S(2)}) async-start(s8[16777216]{0:T(1024)(128)(4,1)} %bitcast.109), calls=%async_computation.8 | async-start | bytes 8388608
  2295.5 9.9 slice-start.2
  2295.6 11.1 slice-start.3
  2306.6 6.2 copy-start.23
Sparse Core Ops, SparseCore 0:
  840.2 44.3 all-reduce.3
  1168.8 1110.2 all-reduce.5
where the time goes:
time: 2340 us; the launch traced here: 2320 us
  waiting for transfers between devices  1220 us (52%)
  local copies, waits for them, and re-layouts  630 us (27%)
  other arithmetic  223 us (10%)
  Pallas kernels  156 us (7%)
  starting transfers between devices  64.4 us (3%)
    psum x1, waiting for transfers between devices, local_step(): grad_gate = lax.psum(grad_gate, 'dp')  728 us
    all_to_all x1, waiting for transfers between devices, local_step(): lax.all_to_all(jnp.where(slot_valid, d_rows[slot_row], 0), 'ep', 0, 0, ti...  178 us
    all_to_all x1, waiting for transfers between devices, local_step(): lax.all_to_all(jnp.where(send_valid, d_out[send_asg], 0), 'ep', 0, 0, til...  169 us
    all_to_all x1, waiting for transfers between devices, local_step(): lax.all_to_all(jnp.where(slot_valid, out_sorted[slot_row], 0), 'ep', 0, 0...  142 us
    another operation x6, Pallas kernels  106 us
    unnamed x82, local copies, waits for them, and re-layouts  70.7 us
    gather x1, local copies, waits for them, and re-layouts, local_step(): within_start[row_src, row_exp]  68.6 us
    unnamed x5, Pallas kernels  50.6 us
  transfers between devices with their start and end apart: 7, of which 5 were waited for; matrix products, arithmetic and copies ran while one was open for 24% of the time, Pallas kernels for 5%

commit v1 on v0

v1 whole, which is shorter than its diff:
```python
import functools

import jax
import jax.numpy as jnp
from jax import lax
from jax.experimental import pallas as pl
from jax.experimental.pallas import tpu as pltpu
from jax.sharding import PartitionSpec as P

F32 = jnp.float32
BF16 = jnp.bfloat16
MESH = pl.DeviceIdType.MESH
VMEM_MAX = 63 * 1024 * 1024
T = 256
NB = 256
HALF = 1024
D = 1024
FF = 512
NE = 8
S = 8
L = 128
Q = 4
RB = 1032
R1 = 8256
R2 = 16448


def dot(a, b, ca=1, cb=0):
    return lax.dot_general(a, b, (((ca,), (cb,)), ((), ())), preferred_element_type=F32)


def vspec():
    return pl.BlockSpec(memory_space=pltpu.VMEM)


def aspec():
    return pl.BlockSpec(memory_space=pl.ANY)


def sspec():
    return pl.BlockSpec(memory_space=pltpu.SMEM)


def barrier_all(dp, ep):
    bar = pltpu.get_barrier_semaphore()
    for k in range(1, S):
        pl.semaphore_signal(bar, inc=1, device_id=((dp + k // Q) % 2, (ep + k % Q) % Q), device_id_type=MESH)
    pl.semaphore_wait(bar, 7)


def gather_kernel(x_ref, r_ref, ids_ref, wr_ref,
                  xon, xof, ron, rof, xqn, rqn, gt_out, idx_out, gat_out, cnt_out,
                  gt_s, pos_s, v_s, ssem, rsem, lsem, gsend, grecv):
    dp = lax.axis_index('dp')
    ep = lax.axis_index('ep')
    c = ep % 2
    xc = ep // 2
    me = dp * Q + ep
    mate = (dp, xc * 2 + 1 - c)
    xnb = (dp, (1 - xc) * 2 + c)
    ynb = (1 - dp, ep)
    barrier_all(dp, ep)

    def rcopy(src, dst, k, dev):
        return pltpu.make_async_remote_copy(src_ref=src, dst_ref=dst, send_sem=ssem.at[k], recv_sem=rsem.at[k], device_id=dev, device_id_type=MESH)

    direct = [
        rcopy(x_ref, xof.at[c], 0, xnb), rcopy(x_ref, xqn.at[c], 1, ynb),
        rcopy(r_ref, rof.at[c], 2, xnb), rcopy(r_ref, rqn.at[c], 3, ynb),
        rcopy(x_ref, xon.at[c], Q, mate), rcopy(r_ref, ron.at[c], 5, mate)]
    for cp in direct:
        cp.start()
    local = [pltpu.make_async_copy(x_ref, xon.at[c], lsem.at[0]), pltpu.make_async_copy(r_ref, ron.at[c], lsem.at[1])]
    for cp in local:
        cp.start()

    zt = dot(wr_ref[...], x_ref[...], 1, 1)
    eio = lax.broadcasted_iota(jnp.int32, (32, NB), 0)
    sel = eio == ids_ref[0:1, :]
    for j in range(1, S):
        sel = sel | (eio == ids_ref[j:j + 1, :])
    zm = jnp.max(jnp.where(sel, zt, -jnp.inf), axis=0, keepdims=True)
    pe = jnp.where(sel, jnp.exp(zt - zm), 0.0)
    gt_s[me] = jnp.where(sel, pe / jnp.sum(pe, axis=0, keepdims=True), -1.0)
    gcopies = []
    for k in range(1, S):
        dev = ((dp + k // Q) % 2, (ep + k % Q) % Q)
        cp = pltpu.make_async_remote_copy(src_ref=gt_s.at[me], dst_ref=gt_s.at[me], send_sem=gsend.at[k - 1], recv_sem=grecv.at[k - 1], device_id=dev, device_id_type=MESH)
        cp.start()
        gcopies.append(cp)
    for cp in gcopies:
        cp.wait()

    tri = (lax.broadcasted_iota(jnp.int32, (NB, NB), 0) < lax.broadcasted_iota(jnp.int32, (NB, NB), 1)).astype(BF16)
    srow = lax.broadcasted_iota(jnp.int32, (S, NB), 0)
    tlan = lax.broadcasted_iota(jnp.int32, (S, NB), 1).astype(F32)
    for half in range(2):
        base = jnp.zeros((S, 1), F32)
        for k in range(Q):
            hd = dp if half == 0 else 1 - dp
            xx = xc if k < 2 else 1 - xc
            g = gt_s[hd * Q + xx * 2 + k % 2, pl.ds(pl.multiple_of(ep * S, S), S), :]
            m = g >= 0.0
            mf = m.astype(F32)
            pos = dot(mf.astype(BF16), tri) + base
            pos_s[half * Q + k] = jnp.where(m, pos, -1.0)
            base = base + jnp.sum(mf, axis=1, keepdims=True)
            g = jnp.where(m, g, 0.0)
            g1 = g.astype(BF16)
            e1 = g - g1.astype(F32)
            g2 = e1.astype(BF16)
            g3 = (e1 - g2.astype(F32)).astype(BF16)
            head = jnp.where(srow == 0, tlan, jnp.where(srow == 1, float(k), 0.0))
            v_s[half * Q + k] = jnp.concatenate([head, g1.astype(F32), g2.astype(F32), g3.astype(F32)], axis=0).astype(BF16)
        cnt_out[half] = jnp.broadcast_to(base, (S, L)).astype(jnp.int32)

    pio = lax.broadcasted_iota(jnp.int32, (NB, NB), 0).astype(F32)
    rio = lax.broadcasted_iota(jnp.int32, (32, NB), 0)
    lio = lax.broadcasted_iota(jnp.int32, (1, NB), 1)

    def list_body(he, carry):
        half = he // S
        e = he % S
        cnt_e = cnt_out[half, pl.ds(e, 1), 0:1]
        for pt in range(Q):
            acc = jnp.zeros((32, NB), F32)
            for k in range(pt, Q):
                prow = pos_s[half * Q + k, pl.ds(e, 1), :] - float(256 * pt)
                oh = (pio == prow).astype(F32).astype(BF16)
                acc = acc + dot(v_s[half * Q + k], oh, 1, 1)
            ids = (acc[0:1, :] + 256.0 * acc[1:2, :]).astype(jnp.int32)
            ids = jnp.where(lio + 256 * pt < cnt_e, ids, HALF)
            gv = jnp.sum(jnp.where((rio >= S) & (rio % S == e), acc, 0.0), axis=0, keepdims=True)
            for q in range(2):
                idx_out[he, 2 * pt + q:2 * pt + q + 1, :] = ids[:, L * q:L * (q + 1)]
                gat_out[he, 2 * pt + q:2 * pt + q + 1, :] = gv[:, L * q:L * (q + 1)]
        return carry

    lax.fori_loop(0, 16, list_body, 0)
    gt_out[...] = gt_s[...]

    fwd = [
        rcopy(xof.at[c], xof.at[c], 6, mate), rcopy(xqn.at[c], xqn.at[c], 7, mate),
        rcopy(rof.at[c], rof.at[c], S, mate), rcopy(rqn.at[c], rqn.at[c], 9, mate)]
    for k in range(Q):
        direct[k].wait_recv()
        fwd[k].start()
    for cp in local:
        cp.wait()
    direct[Q].wait_recv()
    direct[5].wait_recv()
    for cp in direct:
        cp.wait_send()
    for cp in fwd:
        cp.wait()


def load_rows(srcs, dst2, tmp, sem):
    copies = [pltpu.make_async_copy(s, tmp.at[i % 2], sem.at[i % 2]) for i, s in enumerate(srcs)]
    copies[0].start()
    for i in range(len(srcs)):
        if i + 1 < len(srcs):
            copies[i + 1].start()
        copies[i].wait()

        def body(b, carry, i=i):
            r0 = pl.multiple_of(b * 64, 64)
            for s in range(S):
                dst2[pl.ds((i * NB + r0) * S + s, 64, stride=S), :] = tmp[i % 2, pl.ds(r0, 64), L * s:L * (s + 1)].astype(F32)
            return carry

        lax.fori_loop(0, NB // 64, body, 0)


def rows2d(ref2, base):
    return [ref2[pl.ds(base * S + s, T, stride=S), :] for s in range(S)]


def zero_rows(ref2, n):
    def body(i, carry):
        ref2[pl.ds(pl.multiple_of(i * 64, 64), 64), :] = jnp.zeros((64, L), F32)
        return carry
    lax.fori_loop(0, n // 64, body, 0)


def row8(t):
    return pl.ds(pl.multiple_of(t * S, S), S)


def own_kernel(cnt, idx, gat, pid, xn, xf, rn, rf, w1, w3, w2,
               y_out, dx_out, dgt_out,
               x2, r2, u2, rr2, gb, o2, d2, dgs, dgd, tmp, sem):
    e = pl.program_id(0)

    @pl.when(e == 0)
    def _():
        zero_rows(y_out, R1)
        zero_rows(dx_out, R1)
        zero_rows(u2, 1024 * S + 64)
        zero_rows(rr2, 1024 * S + 64)
        dgd[...] = jnp.zeros_like(dgd)
        x2[8192:8256, :] = jnp.zeros((64, L), F32)
        r2[8192:8256, :] = jnp.zeros((64, L), F32)
        load_rows([xn.at[0], xn.at[1], xf.at[0], xf.at[1]], x2, tmp, sem)
        load_rows([rn.at[0], rn.at[1], rf.at[0], rf.at[1]], r2, tmp, sem)

    n = cnt[0, e, 0]
    sio = lax.broadcasted_iota(jnp.int32, (S, L), 0)

    def gather_body(c, carry):
        ih = c // 16
        il = (c % 16) * S
        ts = [idx[e, ih, il + j] for j in range(S)]
        gs = [gat[e, ih, il + j] for j in range(S)]
        xs = [x2[row8(t), :] for t in ts]
        rs = [r2[row8(t), :] for t in ts]
        gv = jnp.full((S, L), gs[0], F32)
        for j in range(1, S):
            gv = jnp.where(sio == j, gs[j], gv)
        for j in range(S):
            u2[row8(c * S + j), :] = xs[j]
            rr2[row8(c * S + j), :] = rs[j]
        gb[row8(c), :] = gv
        return carry

    lax.fori_loop(0, (n + 7) // S, gather_body, 0)

    lane = lax.broadcasted_iota(jnp.int32, (T, L), 1)
    rown = lax.broadcasted_iota(jnp.int32, (T, L), 0)

    def tile_body(k, carry):
        base = k * T
        u = jnp.concatenate([p.astype(BF16) for p in rows2d(u2, base)], axis=1)
        gcol = jnp.where(rown + base < n, gb[pl.ds(pl.multiple_of(base, T), T), :], 0.0)
        do = jnp.concatenate([(p * gcol).astype(BF16) for p in rows2d(rr2, base)], axis=1)
        h1 = dot(u, w1[0])
        h3 = dot(u, w3[0])
        sg = jax.nn.sigmoid(h1)
        sl = h1 * sg
        a = (sl * h3).astype(BF16)
        o = dot(a, w2[0]).astype(BF16).astype(F32)
        da = dot(do, w2[0], 1, 1)
        dh1 = (da * h3 * sg * (1.0 + h1 * (1.0 - sg))).astype(BF16)
        dh3 = (da * sl).astype(BF16)
        dr = (dot(dh1, w1[0], 1, 1) + dot(dh3, w3[0], 1, 1)).astype(BF16).astype(F32)
        acc = jnp.zeros((T, L), F32)
        rp = rows2d(rr2, base)
        for s in range(S):
            os = o[:, L * s:L * (s + 1)]
            o2[pl.ds(s, T, stride=S), :] = os
            d2[pl.ds(s, T, stride=S), :] = dr[:, L * s:L * (s + 1)]
            acc = acc + os * rp[s]
        dgc = jnp.sum(acc, axis=1, keepdims=True)
        dgs[...] = jnp.where(lane == e, dgc, 0.0)

        def scat_body(c, carry2):
            cc = c + base // S
            ih = cc // 16
            il = (cc % 16) * S
            ts = [idx[e, ih, il + j] for j in range(S)]
            gs = [gat[e, ih, il + j] for j in range(S)]
            ys = [y_out[row8(ts[j]), :] + gs[j] * o2[row8(c * S + j), :] for j in range(S)]
            ds = [dx_out[row8(ts[j]), :] + d2[row8(c * S + j), :] for j in range(S)]
            dg8 = dgs[row8(c), :]
            gd = [dgd[pl.ds(ts[j], 1), :] + dg8[j:j + 1, :] for j in range(S)]
            for j in range(S):
                y_out[row8(ts[j]), :] = ys[j]
                dx_out[row8(ts[j]), :] = ds[j]
                dgd[pl.ds(ts[j], 1), :] = gd[j]
            return carry2

        lax.fori_loop(0, (jnp.minimum(n - base, T) + 7) // S, scat_body, 0)
        return carry

    lax.fori_loop(0, (n + T - 1) // T, tile_body, 0)

    @pl.when(e == NE - 1)
    def _():
        xc = pid[1] // 2
        tr = jnp.transpose(dgd[0:HALF, :])
        dgt_out[:, pl.ds(pl.multiple_of(xc * 512, 512), 512)] = tr[0:S, 0:512]
        dgt_out[:, pl.ds(pl.multiple_of(512 - xc * 512, 512), 512)] = tr[0:S, 512:1024]


def pair_kernel(yp, dxp, dgt, ynear, yfar, dnear, dfar, dg_out, rbuf, obuf, dgb, ssem, rsem, lsem, gsend, grecv):
    dp = lax.axis_index('dp')
    ep = lax.axis_index('ep')
    c = ep % 2
    me = dp * Q + ep
    mate = (dp, (ep // 2) * 2 + 1 - c)
    barrier_all(dp, ep)
    parts = [(yp, 4096), (dxp, 4096), (yp, 0), (dxp, 0)]
    outs = [yfar, dfar, ynear, dnear]
    sends, loads = [], []
    for i, (src, base) in enumerate(parts):
        cp = pltpu.make_async_remote_copy(
            src_ref=src.at[pl.ds(pl.multiple_of(base + (1 - c) * 2048, 2048), 2048)], dst_ref=rbuf.at[i],
            send_sem=ssem.at[i], recv_sem=rsem.at[i], device_id=mate, device_id_type=MESH)
        cp.start()
        sends.append(cp)
        ld = pltpu.make_async_copy(src.at[pl.ds(pl.multiple_of(base + c * 2048, 2048), 2048)], obuf.at[i], lsem.at[i])
        ld.start()
        loads.append(ld)
    gcopies = []
    for k in range(1, S):
        dev = ((dp + k // Q) % 2, (ep + k % Q) % Q)
        cp = pltpu.make_async_remote_copy(src_ref=dgt, dst_ref=dgb.at[me], send_sem=gsend.at[k - 1], recv_sem=grecv.at[k - 1], device_id=dev, device_id_type=MESH)
        cp.start()
        gcopies.append(cp)
    for i in range(Q):
        loads[i].wait()
        sends[i].wait_recv()

        def body(b, carry, i=i):
            s = pl.ds(pl.multiple_of(b * L, L), L)
            outs[i][s, :] = obuf[i, s, :] + rbuf[i, s, :]
            return carry

        lax.fori_loop(0, 16, body, 0)
    for cp in gcopies:
        cp.wait()
    for cp in sends:
        cp.wait_send()
    dgb[me] = dgt[...]
    dg_out[...] = dgb[...]


def grad_kernel(cnt, idx, gat, xon, xof, xqn, xqf, ron, rof, rqn, rqf, w1, w3, w2,
                g1, g3, g2, x2, r2, u2, d2, tmp, sem):
    e = pl.program_id(0)

    @pl.when(e == 0)
    def _():
        zero_rows(u2, 2048 * S + 64)
        zero_rows(d2, 2048 * S + 64)
        x2[16384:16448, :] = jnp.zeros((64, L), F32)
        r2[16384:16448, :] = jnp.zeros((64, L), F32)
        load_rows([a.at[i] for a in (xon, xof, xqn, xqf) for i in range(2)], x2, tmp, sem)
        load_rows([a.at[i] for a in (ron, rof, rqn, rqf) for i in range(2)], r2, tmp, sem)

    n0 = cnt[0, e, 0]
    n = n0 + cnt[1, e, 0]

    def gather_half(h):
        def body(c, carry):
            ih = c // 16
            il = (c % 16) * S
            ts = [idx[h * S + e, ih, il + j] + h * HALF for j in range(S)]
            gs = [gat[h * S + e, ih, il + j] for j in range(S)]
            xs = [x2[row8(t), :] for t in ts]
            rs = [r2[row8(t), :] * g for t, g in zip(ts, gs)]
            for j in range(S):
                u2[row8(h * n0 + c * S + j), :] = xs[j]
                d2[row8(h * n0 + c * S + j), :] = rs[j]
            return carry
        lax.fori_loop(0, (cnt[h, e, 0] + 7) // S, body, 0)

    gather_half(0)
    gather_half(1)
    rown = lax.broadcasted_iota(jnp.int32, (T, L), 0)

    def tile(k, first):
        base = k * T
        u = jnp.concatenate([p.astype(BF16) for p in rows2d(u2, base)], axis=1)
        live = rown + base < n
        do = jnp.concatenate([jnp.where(live, p, 0.0).astype(BF16) for p in rows2d(d2, base)], axis=1)
        h1 = dot(u, w1[0])
        h3 = dot(u, w3[0])
        sg = jax.nn.sigmoid(h1)
        sl = h1 * sg
        a = (sl * h3).astype(BF16)
        da = dot(do, w2[0], 1, 1)
        dh1 = (da * h3 * sg * (1.0 + h1 * (1.0 - sg))).astype(BF16)
        dh3 = (da * sl).astype(BF16)
        if first:
            g1[0] = dot(u, dh1, 0, 0)
            g3[0] = dot(u, dh3, 0, 0)
            g2[0] = dot(a, do, 0, 0)
        else:
            g1[0] += dot(u, dh1, 0, 0)
            g3[0] += dot(u, dh3, 0, 0)
            g2[0] += dot(a, do, 0, 0)

    tile(0, True)

    def tile_body(k, carry):
        tile(k, False)
        return carry

    lax.fori_loop(1, (n + T - 1) // T, tile_body, 0)


def final_kernel(pid, x, r, ynear, dnear, yrec, drec, dg, gt, wr, xon, xof, xqn, xqf,
                 y_out, dx_out, dw_out, dz_s):
    dp = pid[0]
    ep = pid[1]
    xc = ep // 2
    for b in range(S):
        gm = jnp.maximum(gt[b], 0.0)
        dgv = dg[32 * (b // Q):32 * (b // Q + 1), NB * (b % Q):NB * (b % Q + 1)]
        s = jnp.sum(gm * dgv, axis=0, keepdims=True)
        dz_s[b] = (gm * (dgv - s)).astype(BF16)
    acc = jnp.zeros((32, D), F32)
    for h, arrs in enumerate(((xon, xof), (xqn, xqf))):
        hd = dp if h == 0 else 1 - dp
        for f, arr in enumerate(arrs):
            xx = xc if f == 0 else 1 - xc
            for c in range(2):
                acc = acc + dot(dz_s[hd * Q + xx * 2 + c], arr[c])
    dw_out[...] = acc
    dxr = dot(dz_s[dp * Q + ep], wr[...], 0, 0)
    for s in range(S):
        cs = slice(L * s, L * (s + 1))
        rows = pl.ds(s, NB, stride=S)
        y_out[:, cs] = x[:, cs].astype(F32) + (ynear[rows, :] + yrec[rows, :])
        dx_out[:, cs] = r[:, cs].astype(F32) + dxr[:, cs] + (dnear[rows, :] + drec[rows, :])


def solution(mesh):
    axes = ('dp', 'ep')
    sds = jax.ShapeDtypeStruct

    def local_step(tokens, w_router, w_gate, w_up, w_down, top_ids, r_proj):
        pid = jnp.stack([lax.axis_index('dp'), lax.axis_index('ep')]).astype(jnp.int32)
        near = sds((2, NB, D), BF16)
        dma = pltpu.SemaphoreType.DMA
        xon, xof, ron, rof, xqn, rqn, gt, idx, gat, cnt = pl.pallas_call(
            gather_kernel,
            out_shape=[near] * 6 + [sds((S, 32, NB), F32), sds((16, S, L), jnp.int32), sds((16, S, L), F32), sds((2, S, L), jnp.int32)],
            in_specs=[vspec()] * Q,
            out_specs=[aspec()] * 6 + [vspec()] * Q,
            scratch_shapes=[pltpu.VMEM((S, 32, NB), F32), pltpu.VMEM((S, S, NB), F32), pltpu.VMEM((S, 32, NB), BF16),
                            dma((10,)), dma((10,)), dma((2,)), dma((7,)), dma((7,))],
            compiler_params=pltpu.CompilerParams(collective_id=0, has_side_effects=True),
            name='k0_gather',
        )(tokens, r_proj, top_ids.T, w_router.T)

        xswap = [(0, 2), (2, 0), (1, 3), (3, 1)]
        xqf = lax.ppermute(xqn, 'ep', xswap)
        rqf = lax.ppermute(rof, 'dp', [(0, 1), (1, 0)])

        wspec = [pl.BlockSpec((1, D, FF), lambda e: (e, 0, 0)), pl.BlockSpec((1, D, FF), lambda e: (e, 0, 0)), pl.BlockSpec((1, FF, D), lambda e: (e, 0, 0))]
        part = sds((R1, L), F32)
        pspec = pl.BlockSpec((R1, L), lambda e: (0, 0))
        yp, dxp, dgt = pl.pallas_call(
            own_kernel,
            grid=(NE,),
            out_shape=[part, part, sds((S, HALF), F32)],
            in_specs=[sspec()] * Q + [aspec()] * Q + wspec,
            out_specs=[pspec, pspec, pl.BlockSpec((S, HALF), lambda e: (0, 0))],
            scratch_shapes=[pltpu.VMEM((R1, L), F32), pltpu.VMEM((R1, L), F32),
                            pltpu.VMEM((R1, L), F32), pltpu.VMEM((R1, L), F32),
                            pltpu.VMEM((RB, L), F32),
                            pltpu.VMEM((T * S, L), F32), pltpu.VMEM((T * S, L), F32),
                            pltpu.VMEM((T, L), F32), pltpu.VMEM((RB, L), F32),
                            pltpu.VMEM((2, NB, D), BF16), dma((2,))],
            compiler_params=pltpu.CompilerParams(vmem_limit_bytes=VMEM_MAX, dimension_semantics=('arbitrary',)),
            cost_estimate=pl.CostEstimate(flops=20 * 10 ** 9, bytes_accessed=40 * 10 ** 6, transcendentals=0),
            name='k1_own',
        )(cnt, idx, gat, pid, xon, xof, ron, rof, w_gate, w_up, w_down)

        quarter = sds((NB * S, L), F32)
        ynear, yfar, dnear, dfar, dg = pl.pallas_call(
            pair_kernel,
            out_shape=[quarter] * Q + [sds((S, S, HALF), F32)],
            in_specs=[aspec(), aspec(), vspec()],
            out_specs=[vspec()] * 5,
            scratch_shapes=[pltpu.VMEM((Q, NB * S, L), F32), pltpu.VMEM((Q, NB * S, L), F32), pltpu.VMEM((S, S, HALF), F32),
                            dma((Q,)), dma((Q,)), dma((Q,)), dma((7,)), dma((7,))],
            compiler_params=pltpu.CompilerParams(collective_id=1, has_side_effects=True),
            name='k2_pair',
        )(yp, dxp, dgt)

        yrec = lax.ppermute(yfar, 'ep', xswap)
        drec = lax.ppermute(dfar, 'ep', xswap)

        gspec = [pl.BlockSpec((1, D, FF), lambda e: (e, 0, 0)), pl.BlockSpec((1, D, FF), lambda e: (e, 0, 0)), pl.BlockSpec((1, FF, D), lambda e: (e, 0, 0))]
        grad_gate, grad_up, grad_down = pl.pallas_call(
            grad_kernel,
            grid=(NE,),
            out_shape=[sds((NE, D, FF), F32), sds((NE, D, FF), F32), sds((NE, FF, D), F32)],
            in_specs=[sspec()] * 3 + [aspec()] * S + wspec,
            out_specs=gspec,
            scratch_shapes=[pltpu.VMEM((R2, L), F32), pltpu.VMEM((R2, L), F32),
                            pltpu.VMEM((R2, L), F32), pltpu.VMEM((R2, L), F32),
                            pltpu.VMEM((2, NB, D), BF16), dma((2,))],
            compiler_params=pltpu.CompilerParams(vmem_limit_bytes=VMEM_MAX, dimension_semantics=('arbitrary',)),
            cost_estimate=pl.CostEstimate(flops=30 * 10 ** 9, bytes_accessed=90 * 10 ** 6, transcendentals=0),
            name='k3_grad',
        )(cnt, idx, gat, xon, xof, xqn, xqf, ron, rof, rqn, rqf, w_gate, w_up, w_down)

        y, dx, dwt = pl.pallas_call(
            final_kernel,
            out_shape=[sds((NB, D), F32), sds((NB, D), F32), sds((32, D), F32)],
            in_specs=[sspec()] + [vspec()] * 13,
            out_specs=[vspec()] * 3,
            scratch_shapes=[pltpu.VMEM((S, 32, NB), BF16)],
            compiler_params=pltpu.CompilerParams(vmem_limit_bytes=VMEM_MAX),
            name='k4_final',
        )(pid, tokens, r_proj, ynear, dnear, yrec, drec, dg.reshape(64, HALF), gt, w_router.T, xon, xof, xqn, xqf)
        return y, dx, grad_gate, grad_up, grad_down, dwt.T

    tok_spec = P(axes, None)
    exp_spec = P('ep', None, None)
    return jax.shard_map(local_step, mesh=mesh, in_specs=(tok_spec, P(), exp_spec, exp_spec, exp_spec, tok_spec, tok_spec), out_specs=(tok_spec, tok_spec, exp_spec, exp_spec, exp_spec, P()), check_vma=False)
```

time: 2340 us -> 251 us (0.11)
  the two profiles are of different devices: /device:TPU:0 before, /device:TPU:1 now
where the time goes in v1:
time: 251 us; the launch traced here: 250 us
  Pallas kernels  245 us (98%)
  starting transfers between devices  3.9 us (2%)
    pallas_call x1, Pallas kernels, local_step(): pl.pallas_call(grad_kernel, grid=(NE,), out_shape=[sds((NE, D, FF), F32),...  101 us
    pallas_call x1, Pallas kernels, local_step(): pl.pallas_call(own_kernel, grid=(NE,), out_shape=[part, part, sds((S, HAL...  81.6 us
    pallas_call x1, Pallas kernels, local_step(): pl.pallas_call(gather_kernel, out_shape=[near] * 6 + [sds((S, 32, NB), F3...  44.9 us
    pallas_call x1, Pallas kernels, local_step(): pl.pallas_call(pair_kernel, out_shape=[quarter] * Q + [sds((S, S, HALF),...  10.8 us
    pallas_call x1, Pallas kernels, local_step(): pl.pallas_call(final_kernel, out_shape=[sds((NB, D), F32), sds((NB, D), F...  6.74 us
  transfers between devices with their start and end apart: 4, of which 0 were waited for; matrix products, arithmetic and copies ran while one was open for 0% of the time, Pallas kernels for 77%

profile of v1, /device:TPU:1, one launch (start us, length us, event | category | flops | bytes accessed | tf_op | source)
XLA Modules:
  0.0 250.2 jit_solution(8973852956615990080)
XLA Ops:
  0.6 44.9 %k0_gather.1 = (bf16[2,256,1024]{2,1,0:T(8,128)(2,1)}, bf16[2,256,1024]{2,1,0:T(8,128)(2,1)}, bf16[2,256,1024]{2,1,0:T(8,128)(2,1)}, bf16[2,256,1024]{2,1,0:T(8,...) custom-call(bf16[256,1024]{1,0:T(8,128)(2,1)} %x.1, ...), custom_call_target="tpu_custom_call" | custom-call | tf_op jit(solution)/shard_map/k0_gather/pallas_call | solution.py:427
  45.5 1.2 collective-permute-start.3
  46.7 1.2 collective-permute-start.2
  47.9 0.7 pad_add_fusion.pid
  48.6 81.6 %k1_own.1 = (f32[8256,128]{1,0:T(8,128)}, f32[8256,128]{1,0:T(8,128)}, f32[8,1024]{1,0:T(8,128)}) custom-call(s32[2,8,128]{2,1,0:T(8,128)} %get-tuple-element.30.cnt, s32[16,8,128]{2,1,0:T(8,128)} %get-tuple-element.31.idx, f32[16,8,128]{2,1,0:T(8,128)} %get-tuple-element.32.gat, s32[2]{0:T(128)} %pad_add_fusion.pid, ...), custom_call_target="tpu_custom_call" | custom-call | flops 20000000000 | bytes 40000000 | tf_op jit(solution)/shard_map/k1_own/pallas_call | solution.py:445
  130.1 10.8 %k2_pair.1 = (f32[2048,128]{1,0:T(8,128)}, f32[2048,128]{1,0:T(8,128)}, f32[2048,128]{1,0:T(8,128)}, f32[2048,128]{1,0:T(8,128)}, f32[8,8,1024]{2,1,0:T(8,128)}) custom-call(f32[8256,128]{1,0:T(8,128)} %get-tuple-element.37.yp, f32[8256,128]{1,0:T(8,128)} %get-tuple-element.38.dxp, f32[8,1024]{1,0:T(8,128)} %get-tuple-element.39.dgt), custom_call_target="tpu_custom_call" | custom-call | tf_op jit(solution)/shard_map/k2_pair/pallas_call | solution.py:463
  141.0 1.2 collective-permute-start
  142.2 0.3 collective-permute-start.1
  142.5 0.0 collective-permute-done.3.rqf
  142.5 0.0 collective-permute-done.2.xqf
  142.5 101.0 %k3_grad.1 = (f32[8,1024,512]{2,1,0:T(8,128)}, f32[8,1024,512]{2,1,0:T(8,128)}, f32[8,512,1024]{2,1,0:T(8,128)}) custom-call(s32[2,8,128]{2,1,0:T(8,128)} %get-tuple-element.30.cnt, s32[16,8,128]{2,1,0:T(8,128)} %get-tuple-element.31.idx, f32[16,8,128]{2,1,0:T(8,128)} %get-tuple-element.32.gat, bf16[2,256,1024]{2,1,0:T(8,128)(2,1)} %get-tuple-element.33.xn.xon, ...), custom_call_target="tpu_custom_call" | custom-call | flops 30000001024 | bytes 90000000 | tf_op jit(solution)/shard_map/k3_grad/pallas_call | solution.py:478
  243.5 0.0 collective-permute-done.yrec
  243.5 0.0 collective-permute-done.1.drec
  243.5 6.7 %k4_final.1 = (f32[256,1024]{1,0:T(8,128)}, f32[256,1024]{1,0:T(8,128)}, f32[32,1024]{1,0:T(8,128)}) custom-call(s32[2]{0:T(128)} %pad_add_fusion.pid, bf16[256,1024]{1,0:T(8,128)(2,1)} %x.1, bf16[256,1024]{1,0:T(8,128)(2,1)} %r.1, f32[2048,128]{1,0:T(8,128)} %get-tuple-element.40.ynear, f32[2048,128]{1,0:T(8,128)} %get-tuple-element.41.dnear, ...), custom_call_target="tpu_custom_call" | custom-call | tf_op jit(solution)/shard_map/k4_final/pallas_call | solution.py:492
Async XLA Ops:
  45.5 97.0 %collective-permute-start.3 = (bf16[2,256,1024]{2,1,0:T(8,128)(2,1)}, bf16[2,256,1024]{2,1,0:T(8,128)(2,1)}, u32[]{:S(2)}, u32[]{:S(2)}) collective-permute-start(bf16[2,256,1024]{2,1,0:T(8,128)(2,1)} %get-tuple-element.36.rf.rof), channel_id=1, source_target_pairs={{0,4},{4,0},{1,5},{5,1},{2,6},{6,2},{3,7},{7,3}} | collective-permute-start | bytes 3145736 | tf_op jit(solution)/shard_map/ppermute | solution.py:440
  46.7 95.7 %collective-permute-start.2 = (bf16[2,256,1024]{2,1,0:T(8,128)(2,1)}, bf16[2,256,1024]{2,1,0:T(8,128)(2,1)}, u32[]{:S(2)}, u32[]{:S(2)}) collective-permute-start(bf16[2,256,1024]{2,1,0:T(8,128)(2,1)} %get-tuple-element.46.xqn), channel_id=1, source_target_pairs={{0,2},{2,0},{1,3},{3,1},{4,6},{6,4},{5,7},{7,5}} | collective-permute-start | bytes 3145736 | tf_op jit(solution)/shard_map/ppermute | solution.py:439
  141.0 102.5 %collective-permute-start = (f32[2048,128]{1,0:T(8,128)}, f32[2048,128]{1,0:T(8,128)}, u32[]{:S(2)}, u32[]{:S(2)}) collective-permute-start(f32[2048,128]{1,0:T(8,128)} %get-tuple-element.42), channel_id=1, source_target_pairs={{0,2},{2,0},{1,3},{3,1},{4,6},{6,4},{5,7},{7,5}} | collective-permute-start | bytes 3145736 | tf_op jit(solution)/shard_map/ppermute | solution.py:474
  142.2 101.3 %collective-permute-start.1 = (f32[2048,128]{1,0:T(8,128)}, f32[2048,128]{1,0:T(8,128)}, u32[]{:S(2)}, u32[]{:S(2)}) collective-permute-start(f32[2048,128]{1,0:T(8,128)} %get-tuple-element.43), channel_id=1, source_target_pairs={{0,2},{2,0},{1,3},{3,1},{4,6},{6,4},{5,7},{7,5}} | collective-permute-start | bytes 3145736 | tf_op jit(solution)/shard_map/ppermute | solution.py:475
